TPU v7x, 32 devices: a whole 2x2x4 slice. The times are simulated.
32 devices in a mesh: seq: 8 (over y, x, core), batch: 4 (over z).
Axes of the slice: x: 2, y: 2, z: 4, core: 2. Of those that a mesh axis runs over, the one named last changes fastest.
Arguments:
- queries: bfloat16 [4096, 4096], P(('batch', 'seq')), parts along dimension 0, may hold values from -6 to 6
- key_vectors: bfloat16 [4096, 4096], P(('batch', 'seq')), parts along dimension 0, may hold values from -6 to 6
- value_vectors: bfloat16 [4096, 4096], P(('batch', 'seq')), parts along dimension 0, may hold values from -6 to 6
- residual_in: bfloat16 [4096, 4096], P(('batch', 'seq')), parts along dimension 0, may hold values from -6 to 6
- input_logit: float32 [8, 4096], P(None, ('batch', 'seq')), parts along dimension 1, may hold values from -8 to 300
- forget_logit: float32 [8, 4096], P(None, ('batch', 'seq')), parts along dimension 1, may hold values from -3 to 13
- mix_gain: float32 [4096], replicated, may hold values from 0.1 to 1.9
- ffn_gain: float32 [4096], replicated, may hold values from 0.1 to 1.9
- expert_gate: bfloat16 [8, 4096, 704], P('seq'), may hold values from -0.09375 to 0.09375
- expert_up: bfloat16 [8, 4096, 704], P('seq'), may hold values from -0.09375 to 0.09375
- expert_down: bfloat16 [8, 704, 4096], P('seq'), may hold values from -0.21875 to 0.21875
- routes: int32 [4096, 2], P(('batch', 'seq')), parts along dimension 0, may hold values from 0 to 7, all different within a row; in each aligned block of 128 rows (0 to 127, 128 to 255, ...) at most 64 rows name the same one
- route_weight: float32 [4096, 2], P(('batch', 'seq')), parts along dimension 0, may hold values from 0.2 to 1
Outputs:
- block_out: bfloat16 [4096, 4096], P(('batch', 'seq')), parts along dimension 0
There are 4 independent parts, one for each index of `batch`. A program takes and returns all parts, laid end to end along the dimension named above; an argument that names none is the same for every part. Nothing has to cross between parts.
Inputs may be any that keep to these rules, and one draw needn't show every extreme that they name: `routes`: each row names two different experts. Within the rows of one device no expert is named by more than 64 rows, and in some device one expert is named by exactly 64 rows.
All inputs are finite; a program needn't handle non-finite values.
Results may differ from a plain program's by a relative error of at most 0.0081.
Values may be sent and summed in bfloat16 or wider, within the bound.
A program may use at most 128 MiB of HBM per device.

v0:
```python
import math

import jax
import jax.numpy as jnp
from jax import lax
from jax.sharding import PartitionSpec as P

NEG_FILL = -1e30
EPSILON = 1e-06


def join_states(earlier, later):
    total_early, state_early, normv_early, peak_early = earlier
    total_late, state_late, normv_late, peak_late = later
    carried = total_late + peak_early
    peak_new = jnp.maximum(carried, peak_late)
    scale_early = jnp.exp(carried - peak_new)
    scale_late = jnp.exp(peak_late - peak_new)
    state_new = scale_early[..., None] * state_early + scale_late[..., None] * state_late
    normv_new = scale_early * normv_early + scale_late * normv_late
    return (total_early + total_late, state_new, normv_new, peak_new)


def block_state(keys_three, values_three, log_forget, input_gate):
    cumul_log = jnp.cumsum(log_forget, axis=1)
    tail_log = cumul_log[:, -1:] - cumul_log + input_gate
    peak_tail = jnp.max(tail_log, axis=1)
    weight = jnp.exp(tail_log - peak_tail[:, None])
    weighted = keys_three.astype(jnp.float32) * jnp.transpose(weight)[:, :, None]
    rounded = weighted.astype(jnp.bfloat16)
    state_mat = jnp.einsum(
        "thd,the->hde", rounded, values_three, preferred_element_type=jnp.float32
    )
    norm_vec = jnp.sum(weighted, axis=0)
    return (
        jnp.broadcast_to(cumul_log[:, -1:], norm_vec.shape),
        state_mat,
        norm_vec,
        jnp.broadcast_to(peak_tail[:, None], norm_vec.shape),
    )


def block_mix(queries_three, keys_three, values_three, log_forget, input_gate, carry_in):
    tokens = queries_three.shape[0]
    inverse_root = 1.0 / math.sqrt(queries_three.shape[2])
    cumul_log = jnp.cumsum(log_forget, axis=1)
    carry_total, carry_state, carry_norm, carry_peak = carry_in
    log_weight = cumul_log[:, :, None] - cumul_log[:, None, :] + input_gate[:, None, :]
    causal = jnp.arange(tokens)[:, None] >= jnp.arange(tokens)[None, :]
    log_weight = jnp.where(causal[None], log_weight, NEG_FILL)
    carried = cumul_log + carry_peak[:, 0:1]
    peak_log = jnp.maximum(jnp.max(log_weight, axis=2), carried)
    decay_mat = jnp.exp(log_weight - peak_log[:, :, None])
    scores = (
        jnp.einsum("thd,shd->hts", queries_three, keys_three, preferred_element_type=jnp.float32)
        * inverse_root
    )
    coef = decay_mat * scores
    denom_sum = jnp.sum(coef, axis=2)
    numer_sum = jnp.einsum(
        "hts,she->the", coef.astype(jnp.bfloat16), values_three, preferred_element_type=jnp.float32
    )
    carry_reach = jnp.exp(carried - peak_log) * inverse_root
    query_float = queries_three.astype(jnp.float32)
    from_state = jnp.einsum(
        "thd,hde->the", query_float, carry_state, precision=lax.Precision.HIGHEST
    )
    from_norm = jnp.einsum("thd,hd->ht", query_float, carry_norm, precision=lax.Precision.HIGHEST)
    numer_sum = numer_sum + jnp.transpose(carry_reach)[:, :, None] * from_state
    denom_sum = denom_sum + carry_reach * from_norm
    floor_sum = jnp.maximum(jnp.abs(denom_sum), 1.0)
    return numer_sum / jnp.transpose(floor_sum)[:, :, None]


def shards(
    queries,
    key_vectors,
    value_vectors,
    residual_in,
    input_logit,
    forget_logit,
    mix_gain,
    ffn_gain,
    expert_gate,
    expert_up,
    expert_down,
    routes,
    route_weight,
):
    tokens, model_width = queries.shape
    head_count = input_logit.shape[0]
    head_dim = model_width // head_count
    devices = lax.axis_size("seq")
    queries_three = queries.reshape(tokens, head_count, head_dim)
    keys_three = key_vectors.reshape(tokens, head_count, head_dim)
    group = devices // head_count
    group_width = model_width // devices
    query_send = jnp.repeat(queries_three, group, axis=1)
    key_send = jnp.repeat(keys_three, group, axis=1)
    value_send = value_vectors.reshape(tokens, devices, group_width)
    query_all, key_all, value_all = (
        lax.all_to_all(query_send, "seq", split_axis=1, concat_axis=0, tiled=True),
        lax.all_to_all(key_send, "seq", split_axis=1, concat_axis=0, tiled=True),
        lax.all_to_all(value_send, "seq", split_axis=1, concat_axis=0, tiled=True),
    )
    input_all, forget_all = (
        lax.all_gather(input_logit, "seq", axis=1, tiled=True),
        lax.all_gather(forget_logit, "seq", axis=1, tiled=True),
    )
    head_index = lax.axis_index("seq") // group
    input_head = lax.dynamic_slice_in_dim(input_all, head_index, 1, 0)
    forget_head = jax.nn.log_sigmoid(lax.dynamic_slice_in_dim(forget_all, head_index, 1, 0))

    def per_block(array):
        return array.reshape((devices, tokens) + array.shape[1:])

    def per_gate(array):
        return jnp.transpose(array.reshape(1, devices, tokens), (1, 0, 2))

    start = (
        jnp.zeros((1, head_dim), jnp.float32),
        jnp.zeros((1, head_dim, group_width), jnp.float32),
        jnp.zeros((1, head_dim), jnp.float32),
        jnp.full((1, head_dim), NEG_FILL, jnp.float32),
    )

    def advance(carry_in, pieces):
        query_block, key_block, value_block, forget_block, input_block = pieces
        result = block_mix(query_block, key_block, value_block, forget_block, input_block, carry_in)
        carry_out = join_states(
            carry_in, block_state(key_block, value_block, forget_block, input_block)
        )
        return (carry_out, result)

    unused, mixed = lax.scan(
        advance,
        start,
        (
            per_block(query_all),
            per_block(key_all),
            per_block(value_all),
            per_gate(forget_head),
            per_gate(input_head),
        ),
    )
    mixed = mixed.reshape(devices * tokens, 1, group_width)
    mixer_out = lax.all_to_all(mixed, "seq", split_axis=0, concat_axis=1, tiled=True).reshape(
        tokens, model_width
    )
    mixer_square = jnp.mean(mixer_out * mixer_out, axis=1, keepdims=True)
    updated = (
        residual_in.astype(jnp.float32) + mixer_out * lax.rsqrt(mixer_square + EPSILON) * mix_gain
    ).astype(jnp.bfloat16)
    updated_float = updated.astype(jnp.float32)
    updated_square = jnp.mean(updated_float * updated_float, axis=1, keepdims=True)
    normed = (updated_float * lax.rsqrt(updated_square + EPSILON) * ffn_gain).astype(jnp.bfloat16)
    capacity = 4 * tokens // devices
    flat_routes = routes.reshape(-1)
    matches = (flat_routes[:, None] == jnp.arange(devices, dtype=jnp.int32)[None, :]).astype(
        jnp.int32
    )
    before = jnp.cumsum(matches, axis=0) - matches
    position = jnp.sum(before * matches, axis=1)
    slot_index = (flat_routes * capacity + position).reshape(tokens, 2)
    columns = jnp.arange(devices * capacity, dtype=jnp.int32)
    pick_first = (slot_index[:, 0:1] == columns[None, :]).astype(jnp.bfloat16)
    pick_second = (slot_index[:, 1:2] == columns[None, :]).astype(jnp.bfloat16)
    spread = jnp.einsum(
        "tc,td->cd", pick_first + pick_second, normed, preferred_element_type=jnp.float32
    ).astype(jnp.bfloat16)
    outbound = spread.reshape(devices, capacity, model_width)
    block_in = lax.all_to_all(outbound, "seq", split_axis=0, concat_axis=0, tiled=True)
    row_block = block_in.reshape(-1, model_width)
    gate_val = jnp.dot(row_block, expert_gate[0], preferred_element_type=jnp.float32)
    up_val = jnp.dot(row_block, expert_up[0], preferred_element_type=jnp.float32)
    hidden = (jax.nn.silu(gate_val) * up_val).astype(jnp.bfloat16)
    result = jnp.dot(hidden, expert_down[0], preferred_element_type=jnp.float32).astype(
        jnp.bfloat16
    )
    inbound = lax.all_to_all(
        result.reshape(block_in.shape), "seq", split_axis=0, concat_axis=0, tiled=True
    )
    flat_back = inbound.reshape(devices * capacity, model_width)
    first_out = jnp.dot(pick_first, flat_back, preferred_element_type=jnp.float32)
    second_out = jnp.dot(pick_second, flat_back, preferred_element_type=jnp.float32)
    expert_mix = route_weight[:, 0:1] * first_out + route_weight[:, 1:2] * second_out
    return (updated_float + expert_mix).astype(jnp.bfloat16)


def solution(mesh):
    return jax.shard_map(
        shards,
        mesh=mesh,
        in_specs=(
            P(("batch", "seq"), None),
            P(("batch", "seq"), None),
            P(("batch", "seq"), None),
            P(("batch", "seq"), None),
            P(None, ("batch", "seq")),
            P(None, ("batch", "seq")),
            P(),
            P(),
            P("seq", None, None),
            P("seq", None, None),
            P("seq", None, None),
            P(("batch", "seq"), None),
            P(("batch", "seq"), None),
        ),
        out_specs=P(("batch", "seq"), None),
        check_vma=False,
    )
```

profile of v0, /device:TPU:0, one launch (start us, length us, event | category | flops | bytes accessed | tf_op | source)
XLA Modules:
  0.0 361.2 jit_solution(481874486688636953)
XLA Ops:
  0.0 2.3 copy.82
  2.3 5.2 %all-to-all-start = ((bf16[128,8,512]{0,2,1:T(8,128)(2,1)}), bf16[128,8,512]{0,2,1:T(8,128)(2,1)S(1)}, u32[]{:S(2)}, u32[]{:S(2)}) async-start(bf16[128,8,512]{0,2,1:T(8,128)(2,1)} %bitcast.2), calls=%async_computation | async-start | bytes 2097152 | tf_op jit(solution)/shard_map/all_to_all | solution.py:103
  8.9 14.1 %all-to-all-done = bf16[128,8,512]{0,2,1:T(8,128)(2,1)S(1)} async-done(((bf16[128,8,512]{0,2,1:T(8,128)(2,1)}), bf16[128,8,512]{0,2,1:T(8,128)(2,1)S(1)}, u32[]{:S(2)}, u32[]{:S(2)}) %all-to-all-start) | async-done | bytes 1048608 | tf_op jit(solution)/shard_map/all_to_all | solution.py:103
  22.9 3.6 all-to-all-start.1
  27.8 14.0 %all-to-all-done.1 = bf16[128,8,512]{0,2,1:T(8,128)(2,1)S(1)} async-done(((bf16[128,8,512]{0,2,1:T(8,128)(2,1)}), bf16[128,8,512]{0,2,1:T(8,128)(2,1)S(1)}, u32[]{:S(2)}, u32[]{:S(2)}) %all-to-all-start.1) | async-done | bytes 1048608 | tf_op jit(solution)/shard_map/all_to_all | solution.py:104
  41.8 4.2 %all-to-all-start.2 = ((bf16[128,8,512]{0,2,1:T(8,128)(2,1)}), bf16[128,8,512]{0,2,1:T(8,128)(2,1)}, u32[]{:S(2)}, u32[]{:S(2)}) async-start(bf16[128,8,512]{0,2,1:T(8,128)(2,1)} %bitcast.8), calls=%async_computation.2 | async-start | bytes 2097152 | tf_op jit(solution)/shard_map/all_to_all | solution.py:102
  46.1 18.5 %all_gather.7 = f32[8,1024]{1,0:T(8,128)S(1)} all-gather(f32[8,128]{1,0:T(8,128)S(1)} %copy-done.9), channel_id=1, replica_groups=mesh['seq'=8,'batch'=4] {'seq'}, dimensions={1}, use_global_device_ids=true | all-gather | bytes 36864 | tf_op jit(solution)/shard_map/all_gather | solution.py:107
  64.6 8.2 %all_gather.6 = f32[8,1024]{1,0:T(8,128)S(1)} all-gather(f32[8,128]{1,0:T(8,128)S(1)} %copy-done.10), channel_id=1, replica_groups=mesh['seq'=8,'batch'=4] {'seq'}, dimensions={1}, use_global_device_ids=true | all-gather | bytes 36864 | tf_op jit(solution)/shard_map/all_gather | solution.py:108
  79.3 2.7 copy.87
  82.0 2.5 copy.90
  84.5 105.7 %while.17 = (s32[]{:T(128)}, f32[1,512,512]{2,1,0:T(8,128)S(1)}, f32[1,512]{1,0:T(1,128)S(1)}, f32[1,512]{1,0:T(1,128)S(1)}, f32[8,128,1,512]{3,1,0,2:T(8,128)},...) while((s32[]{:T(128)}, f32[1,512,512]{2,1,0:T(8,128)S(1)}, ...), condition=%wide.region_6.7_spmd.clone, body=%wide.region_0.6_spmd.clone.sunk | while | flops 506255232 | bytes 14530822 | solution.py:135
  93.3 2.0 fusion.120
  119.7 2.0 fusion.120
  132.9 2.0 fusion.120
  190.2 5.0 %copy.92 = f32[1024,1,512]{2,1,0:T(1,128)} copy(f32[1024,1,512]{2,0,1:T(8,128)} %bitcast.226) | data formatting | bytes 4194304 | tf_op jit(solution)/shard_map/reshape | solution.py:146
  195.2 3.9 %all-to-all-start.3 = ((f32[1024,1,512]{2,1,0:T(1,128)}), f32[1024,1,512]{2,1,0:T(1,128)S(1)}, u32[]{:S(2)}, u32[]{:S(2)}) async-start(f32[1024,1,512]{2,1,0:T(1,128)} %copy.92), calls=%async_computation.3 | async-start | bytes 4194304 | tf_op jit(solution)/shard_map/all_to_all | solution.py:147
  200.7 24.8 %all-to-all-done.3 = f32[1024,1,512]{2,1,0:T(1,128)S(1)} async-done(((f32[1024,1,512]{2,1,0:T(1,128)}), f32[1024,1,512]{2,1,0:T(1,128)S(1)}, u32[]{:S(2)}, u32[]{:S(2)}) %all-to-all-start.3) | async-done | bytes 2097184 | tf_op jit(solution)/shard_map/all_to_all | solution.py:147
  229.3 51.7 %all_to_all.70 = bf16[8,64,4096]{2,1,0:T(8,128)(2,1)S(1)} all-to-all(bf16[8,64,4096]{2,1,0:T(8,128)(2,1)S(1)} %bitcast.216), channel_id=1, replica_groups=mesh['seq'=8,'batch'=4] {'seq'}, dimensions={0} | all-to-all | bytes 8388608 | tf_op jit(solution)/shard_map/all_to_all | solution.py:172
  282.9 3.2 fusion.50
  286.1 14.1 %convolution_convert_fusion.1 = bf16[512,4096]{1,0:T(8,128)(2,1)} fusion(bf16[1,704,4096]{2,1,0:T(8,128)(2,1)} %param.25, bf16[512,4096]{1,0:T(8,128)(2,1)} %bitcast.222, bf16[1,4096,704]{1,2,0:T(8,128)(2,1)} %param.24, f32[512,704]{0,1:T(8,128)S(1)} %fusion.50), kind=kOutput, calls=%fused_computation.70 | convolution fusion | flops 5909839872 | bytes 21364736 | tf_op jit(solution)/shard_map/dot_general | solution.py:177
  300.2 4.7 %all-to-all-start.5 = ((bf16[8,64,4096]{2,1,0:T(8,128)(2,1)}), bf16[8,64,4096]{2,1,0:T(8,128)(2,1)}, u32[]{:S(2)}, u32[]{:S(2)}) async-start(bf16[8,64,4096]{2,1,0:T(8,128)(2,1)} %bitcast.220), calls=%async_computation.5 | async-start | bytes 8388608 | tf_op jit(solution)/shard_map/all_to_all | solution.py:180
  304.9 49.1 %all-to-all-done.5 = bf16[8,64,4096]{2,1,0:T(8,128)(2,1)} async-done(((bf16[8,64,4096]{2,1,0:T(8,128)(2,1)}), bf16[8,64,4096]{2,1,0:T(8,128)(2,1)}, u32[]{:S(2)}, u32[]{:S(2)}) %all-to-all-start.5) | async-done | bytes 4194336 | tf_op jit(solution)/shard_map/all_to_all | solution.py:180
  354.0 2.9 convolution_multiply_fusion.3
  356.9 4.2 %fusion.54 = bf16[128,4096]{1,0:T(8,128)(2,1)} fusion(f32[128,4096]{1,0:T(8,128)S(1)} %convolution_multiply_fusion.3, bf16[512,4096]{1,0:T(8,128)(2,1)} %bitcast.24, bf16[128,4096]{1,0:T(8,128)(2,1)S(1)} %get-tuple-element.169, f32[128]{0:T(128)S(1)} %get-tuple-element.174, s32[128]{0:T(128)S(1)} %get-tuple-element.177), kind=kOutput, calls=%fused_computation.80 | convolution fusion | flops 539557888 | bytes 8389632 | tf_op jit(solution)/shard_map/dot_general | solution.py:185
  (232 shorter events, 115.3 us)
Async XLA Ops:
  0.0 7.6 %copy-start.4 = (bf16[128,4096]{1,0:T(8,128)(2,1)S(1)}, bf16[128,4096]{1,0:T(8,128)(2,1)}, u32[]{:S(2)}) copy-start(bf16[128,4096]{1,0:T(8,128)(2,1)} %param.17) | copy-start | bytes 3145732
  2.3 20.6 %all-to-all-start = ((bf16[128,8,512]{0,2,1:T(8,128)(2,1)}), bf16[128,8,512]{0,2,1:T(8,128)(2,1)S(1)}, u32[]{:S(2)}, u32[]{:S(2)}) async-start(bf16[128,8,512]{0,2,1:T(8,128)(2,1)} %bitcast.2), calls=%async_computation | async-start | bytes 2097152 | tf_op jit(solution)/shard_map/all_to_all | solution.py:103
  8.9 17.6 %copy-start.5 = (bf16[128,4096]{1,0:T(8,128)(2,1)S(1)}, bf16[128,4096]{1,0:T(8,128)(2,1)}, u32[]{:S(2)}) copy-start(bf16[128,4096]{1,0:T(8,128)(2,1)} %param.15) | copy-start | bytes 3145732
  22.9 18.9 %all-to-all-start.1 = ((bf16[128,8,512]{0,2,1:T(8,128)(2,1)}), bf16[128,8,512]{0,2,1:T(8,128)(2,1)S(1)}, u32[]{:S(2)}, u32[]{:S(2)}) async-start(bf16[128,8,512]{0,2,1:T(8,128)(2,1)} %bitcast.5), calls=%async_computation.1 | async-start | bytes 2097152 | tf_op jit(solution)/shard_map/all_to_all | solution.py:104
  26.5 19.6 %copy-start.9 = (f32[8,128]{1,0:T(8,128)S(1)}, f32[8,128]{1,0:T(8,128)}, u32[]{:S(2)}) copy-start(f32[8,128]{1,0:T(8,128)} %param.19) | copy-start | bytes 12292
  26.5 38.1 %copy-start.10 = (f32[8,128]{1,0:T(8,128)S(1)}, f32[8,128]{1,0:T(8,128)}, u32[]{:S(2)}) copy-start(f32[8,128]{1,0:T(8,128)} %param.20) | copy-start | bytes 12292
  41.8 37.5 %all-to-all-start.2 = ((bf16[128,8,512]{0,2,1:T(8,128)(2,1)}), bf16[128,8,512]{0,2,1:T(8,128)(2,1)}, u32[]{:S(2)}, u32[]{:S(2)}) async-start(bf16[128,8,512]{0,2,1:T(8,128)(2,1)} %bitcast.8), calls=%async_computation.2 | async-start | bytes 2097152 | tf_op jit(solution)/shard_map/all_to_all | solution.py:102
  84.5 8.8 %copy-start = (bf16[8,128,1,512]{3,1,2,0:T(8,128)(2,1)}, bf16[8,128,1,512]{3,1,2,0:T(8,128)(2,1)S(1)}, u32[]{:S(2)}) copy-start(bf16[8,128,1,512]{3,1,2,0:T(8,128)(2,1)S(1)} %get-tuple-element.297) | copy-start | bytes 3145732 | tf_op jit(solution)/shard_map/while
  96.1 1.5 copy-start.1
  97.7 8.8 %copy-start = (bf16[8,128,1,512]{3,1,2,0:T(8,128)(2,1)}, bf16[8,128,1,512]{3,1,2,0:T(8,128)(2,1)S(1)}, u32[]{:S(2)}) copy-start(bf16[8,128,1,512]{3,1,2,0:T(8,128)(2,1)S(1)} %get-tuple-element.297) | copy-start | bytes 3145732 | tf_op jit(solution)/shard_map/while
  110.9 8.8 %copy-start = (bf16[8,128,1,512]{3,1,2,0:T(8,128)(2,1)}, bf16[8,128,1,512]{3,1,2,0:T(8,128)(2,1)S(1)}, u32[]{:S(2)}) copy-start(bf16[8,128,1,512]{3,1,2,0:T(8,128)(2,1)S(1)} %get-tuple-element.297) | copy-start | bytes 3145732 | tf_op jit(solution)/shard_map/while
  122.5 1.5 copy-start.1
  124.1 8.8 %copy-start = (bf16[8,128,1,512]{3,1,2,0:T(8,128)(2,1)}, bf16[8,128,1,512]{3,1,2,0:T(8,128)(2,1)S(1)}, u32[]{:S(2)}) copy-start(bf16[8,128,1,512]{3,1,2,0:T(8,128)(2,1)S(1)} %get-tuple-element.297) | copy-start | bytes 3145732 | tf_op jit(solution)/shard_map/while
  137.3 8.9 %copy-start = (bf16[8,128,1,512]{3,1,2,0:T(8,128)(2,1)}, bf16[8,128,1,512]{3,1,2,0:T(8,128)(2,1)S(1)}, u32[]{:S(2)}) copy-start(bf16[8,128,1,512]{3,1,2,0:T(8,128)(2,1)S(1)} %get-tuple-element.297) | copy-start | bytes 3145732 | tf_op jit(solution)/shard_map/while
  150.5 8.8 %copy-start = (bf16[8,128,1,512]{3,1,2,0:T(8,128)(2,1)}, bf16[8,128,1,512]{3,1,2,0:T(8,128)(2,1)S(1)}, u32[]{:S(2)}) copy-start(bf16[8,128,1,512]{3,1,2,0:T(8,128)(2,1)S(1)} %get-tuple-element.297) | copy-start | bytes 3145732 | tf_op jit(solution)/shard_map/while
  163.8 8.8 %copy-start = (bf16[8,128,1,512]{3,1,2,0:T(8,128)(2,1)}, bf16[8,128,1,512]{3,1,2,0:T(8,128)(2,1)S(1)}, u32[]{:S(2)}) copy-start(bf16[8,128,1,512]{3,1,2,0:T(8,128)(2,1)S(1)} %get-tuple-element.297) | copy-start | bytes 3145732 | tf_op jit(solution)/shard_map/while
  177.0 8.8 %copy-start = (bf16[8,128,1,512]{3,1,2,0:T(8,128)(2,1)}, bf16[8,128,1,512]{3,1,2,0:T(8,128)(2,1)S(1)}, u32[]{:S(2)}) copy-start(bf16[8,128,1,512]{3,1,2,0:T(8,128)(2,1)S(1)} %get-tuple-element.297) | copy-start | bytes 3145732 | tf_op jit(solution)/shard_map/while
  195.2 3.9 %copy-start.8 = (s32[128,2]{0,1:T(2,128)S(1)}, s32[128,2]{0,1:T(2,128)}, u32[]{:S(2)}) copy-start(s32[128,2]{0,1:T(2,128)} %param.26) | copy-start | bytes 3076
  195.2 30.3 %all-to-all-start.3 = ((f32[1024,1,512]{2,1,0:T(1,128)}), f32[1024,1,512]{2,1,0:T(1,128)S(1)}, u32[]{:S(2)}, u32[]{:S(2)}) async-start(f32[1024,1,512]{2,1,0:T(1,128)} %copy.92), calls=%async_computation.3 | async-start | bytes 4194304 | tf_op jit(solution)/shard_map/all_to_all | solution.py:147
  227.9 55.0 %slice-start = ((s8[5767168]{0:T(1024)(128)(4,1)}), s8[4194304]{0:T(1024)(128)(4,1)S(1)}, s32[]{:S(2)}) async-start(s8[5767168]{0:T(1024)(128)(4,1)} %bitcast.232), calls=%async_computation.6 | async-start | bytes 8388608
  229.3 53.6 %slice-start.1 = ((s8[5767168]{0:T(1024)(128)(4,1)}), s8[1572864]{0:T(1024)(128)(4,1)S(1)}, s32[]{:S(2)}) async-start(s8[5767168]{0:T(1024)(128)(4,1)} %bitcast.232), calls=%async_computation.7 | async-start | bytes 3145728
  281.0 2.0 copy-start.2
  300.2 4.7 %copy-start.11 = (f32[128,2]{0,1:T(2,128)S(1)}, f32[128,2]{0,1:T(2,128)}, u32[]{:S(2)}) copy-start(f32[128,2]{0,1:T(2,128)} %param.27) | copy-start | bytes 3076
  300.2 53.8 %all-to-all-start.5 = ((bf16[8,64,4096]{2,1,0:T(8,128)(2,1)}), bf16[8,64,4096]{2,1,0:T(8,128)(2,1)}, u32[]{:S(2)}, u32[]{:S(2)}) async-start(bf16[8,64,4096]{2,1,0:T(8,128)(2,1)} %bitcast.220), calls=%async_computation.5 | async-start | bytes 8388608 | tf_op jit(solution)/shard_map/all_to_all | solution.py:180
  (9 other events, 12.2 us)
where the time goes:
time: 363 us; the launch traced here: 361 us
  waiting for transfers between devices  102 us (28%)
  blocking collectives  78.4 us (22%)
  matrix products  72.6 us (20%)
  local copies, waits for them, and re-layouts  42.9 us (12%)
  other arithmetic  42.8 us (12%)
  starting transfers between devices  21.6 us (6%)
    all_to_all x1, blocking collectives, shards(): lax.all_to_all(outbound, 'seq', split_axis=0, concat_axis=0, tiled=True)  51.7 us
    all_to_all x1, waiting for transfers between devices, shards(): lax.all_to_all(result.reshape(block_in.shape), 'seq', split_axis=0, conca...  49.1 us
    all_to_all x1, waiting for transfers between devices, shards(): lax.all_to_all(mixed, 'seq', split_axis=0, concat_axis=1, tiled=True)  24.8 us
    all_gather x1, blocking collectives, shards(): lax.all_gather(input_logit, 'seq', axis=1, tiled=True)  18.5 us
    dot_general x8, matrix products, block_mix(): jnp.einsum('thd,hde->the', query_float, carry_state, precision=lax.Precis...  15.8 us
    dot_general x1, matrix products, shards(): jnp.dot(hidden, expert_down[0], preferred_element_type=jnp.float32)  14.1 us
    unnamed x33, local copies, waits for them, and re-layouts  14.1 us
    all_to_all x1, waiting for transfers between devices, shards(): lax.all_to_all(key_send, 'seq', split_axis=1, concat_axis=0, tiled=True)  14.1 us
  transfers between devices with their start and end apart: 5, of which 4 were waited for; matrix products, arithmetic and copies ran while one was open for 3% of the time, Pallas kernels for 0%

commit v1 on v0

v1 whole, which is shorter than its diff:
```python
import math

import jax
import jax.numpy as jnp
from jax import lax
from jax.sharding import PartitionSpec as P

EPSILON = 1e-06


def three_parts(array):
    high = lax.reduce_precision(array, 8, 7)
    rest = array - high
    middle = lax.reduce_precision(rest, 8, 7)
    low = rest - middle
    return [part.astype(jnp.bfloat16) for part in (high, middle, low)]


def head_mix(query, key, value, input_gate, forget_gate):
    positions, head_dim = query.shape
    cumul_log = jnp.cumsum(jax.nn.log_sigmoid(forget_gate))
    level = input_gate - cumul_log
    top = lax.cummax(level, axis=0)
    scores = lax.dot_general(
        query, key, (((1,), (1,)), ((), ())), preferred_element_type=jnp.float32
    )
    causal = jnp.arange(positions)[:, None] >= jnp.arange(positions)[None, :]
    decay = jnp.exp(jnp.minimum(level[None, :] - top[:, None], 0.0))
    coef = jnp.where(causal, decay * scores, 0.0) * (1.0 / math.sqrt(head_dim))
    denom_sum = jnp.sum(coef, axis=1, keepdims=True)
    numer_sum = jnp.dot(coef.astype(jnp.bfloat16), value, preferred_element_type=jnp.float32)
    return numer_sum / jnp.maximum(jnp.abs(denom_sum), 1.0)


def shards(
    queries,
    key_vectors,
    value_vectors,
    residual_in,
    input_logit,
    forget_logit,
    mix_gain,
    ffn_gain,
    expert_gate,
    expert_up,
    expert_down,
    routes,
    route_weight,
):
    tokens, model_width = queries.shape
    head_count = input_logit.shape[0]
    head_dim = model_width // head_count
    devices = lax.axis_size("seq")
    group = devices // head_count
    group_width = model_width // devices

    def by_head(array):
        moved = jnp.transpose(array.reshape(tokens, head_count, head_dim), (1, 0, 2))
        return jnp.repeat(moved, group, axis=0)

    gates = jnp.stack(three_parts(input_logit) + three_parts(forget_logit), axis=2)
    gates = jnp.pad(jnp.repeat(gates, group, axis=0), ((0, 0), (0, 0), (0, 122)))
    send = jnp.concatenate(
        (
            by_head(queries),
            by_head(key_vectors),
            jnp.transpose(value_vectors.reshape(tokens, devices, group_width), (1, 0, 2)),
            gates,
        ),
        axis=2,
    )
    got = lax.all_to_all(send, "seq", split_axis=0, concat_axis=0, tiled=True)
    got = got.reshape(devices * tokens, -1)
    gate_parts = got[:, 2 * head_dim + group_width :].astype(jnp.float32)
    mixed = head_mix(
        got[:, :head_dim],
        got[:, head_dim : 2 * head_dim],
        got[:, 2 * head_dim : 2 * head_dim + group_width],
        gate_parts[:, 0] + gate_parts[:, 1] + gate_parts[:, 2],
        gate_parts[:, 3] + gate_parts[:, 4] + gate_parts[:, 5],
    ).astype(jnp.bfloat16)
    mixer_out = lax.all_to_all(
        mixed.reshape(devices, tokens, group_width), "seq", split_axis=0, concat_axis=0, tiled=True
    )
    mixer_out = jnp.transpose(mixer_out, (1, 0, 2)).reshape(tokens, model_width)
    mixer_out = mixer_out.astype(jnp.float32)
    mixer_square = jnp.mean(mixer_out * mixer_out, axis=1, keepdims=True)
    updated = (
        residual_in.astype(jnp.float32) + mixer_out * lax.rsqrt(mixer_square + EPSILON) * mix_gain
    ).astype(jnp.bfloat16)
    updated_float = updated.astype(jnp.float32)
    updated_square = jnp.mean(updated_float * updated_float, axis=1, keepdims=True)
    normed = (updated_float * lax.rsqrt(updated_square + EPSILON) * ffn_gain).astype(jnp.bfloat16)
    capacity = 4 * tokens // devices
    flat_routes = routes.reshape(-1)
    matches = (flat_routes[:, None] == jnp.arange(devices, dtype=jnp.int32)[None, :]).astype(
        jnp.int32
    )
    before = jnp.cumsum(matches, axis=0) - matches
    position = jnp.sum(before * matches, axis=1)
    slot_index = (flat_routes * capacity + position).reshape(tokens, 2)
    columns = jnp.arange(devices * capacity, dtype=jnp.int32)
    pick_first = (slot_index[:, 0:1] == columns[None, :]).astype(jnp.bfloat16)
    pick_second = (slot_index[:, 1:2] == columns[None, :]).astype(jnp.bfloat16)
    spread = jnp.einsum(
        "tc,td->cd", pick_first + pick_second, normed, preferred_element_type=jnp.float32
    ).astype(jnp.bfloat16)
    outbound = spread.reshape(devices, capacity, model_width)
    block_in = lax.all_to_all(outbound, "seq", split_axis=0, concat_axis=0, tiled=True)
    row_block = block_in.reshape(-1, model_width)
    gate_val = jnp.dot(row_block, expert_gate[0], preferred_element_type=jnp.float32)
    up_val = jnp.dot(row_block, expert_up[0], preferred_element_type=jnp.float32)
    hidden = (jax.nn.silu(gate_val) * up_val).astype(jnp.bfloat16)
    result = jnp.dot(hidden, expert_down[0], preferred_element_type=jnp.float32).astype(
        jnp.bfloat16
    )
    inbound = lax.all_to_all(
        result.reshape(block_in.shape), "seq", split_axis=0, concat_axis=0, tiled=True
    )
    flat_back = inbound.reshape(devices * capacity, model_width)
    first_out = jnp.dot(pick_first, flat_back, preferred_element_type=jnp.float32)
    second_out = jnp.dot(pick_second, flat_back, preferred_element_type=jnp.float32)
    expert_mix = route_weight[:, 0:1] * first_out + route_weight[:, 1:2] * second_out
    return (updated_float + expert_mix).astype(jnp.bfloat16)


def solution(mesh):
    return jax.shard_map(
        shards,
        mesh=mesh,
        in_specs=(
            P(("batch", "seq"), None),
            P(("batch", "seq"), None),
            P(("batch", "seq"), None),
            P(("batch", "seq"), None),
            P(None, ("batch", "seq")),
            P(None, ("batch", "seq")),
            P(),
            P(),
            P("seq", None, None),
            P("seq", None, None),
            P("seq", None, None),
            P(("batch", "seq"), None),
            P(("batch", "seq"), None),
        ),
        out_specs=P(("batch", "seq"), None),
        check_vma=False,
    )
```

time: 363 us -> 224 us (0.62)
  matrix products: 72.6 us -> 31.2 us
  waiting for transfers between devices: 102 us -> 62.8 us
  other arithmetic: 42.8 us -> 7.31 us
  local copies, waits for them, and re-layouts: 42.9 us -> 15.9 us
  blocking collectives: 78.4 us -> 97.5 us
  starting transfers between devices: 21.6 us -> 8.24 us
    all_to_all x0 -> x1, blocking collectives: none -> 45.8 us  [shards(): got = lax.all_to_all(send, 'seq', split_axis=0, concat_axis=0, tiled=True)]
    dot_general x40 -> x2, matrix products: 46.7 us -> 3.78 us  [the longest x1 2.43 us: head_mix(): jnp.dot(coef.astype(jnp.bfloat16), value, preferred_element_type=jnp.floa...]
    all_to_all x4 -> x1, waiting for transfers between devices: 52.8 us -> 13.7 us  [shards(): lax.all_to_all(mixed.reshape(devices, tokens, group_width), 'seq', split_...]
    all_gather x2 -> x0, blocking collectives: 26.7 us -> none  [the longest x1 18.5 us: shards(): lax.all_gather(input_logit, 'seq', axis=1, tiled=True)]
    all_to_all x4 -> x1, starting transfers between devices: 16.9 us -> 3.56 us  [shards(): lax.all_to_all(mixed.reshape(devices, tokens, group_width), 'seq', split_...]
    reduce_max x16 -> x0, other arithmetic: 11.7 us -> none  [the longest x8 10.4 us: block_state(): peak_tail = jnp.max(tail_log, axis=1)]
    add x8 -> x0, other arithmetic: 10.3 us -> none  [join_states(): normv_new = scale_early * normv_early + scale_late * normv_late]
    exp x8 -> x0, other arithmetic: 10.2 us -> none  [block_state(): weight = jnp.exp(tail_log - peak_tail[:, None])]
  transfers between devices with their start and end apart: 5 -> 2, of which waited for: 4 -> 2; matrix products, arithmetic and copies ran while one was open for 3% -> 1% of each run, Pallas kernels for 0% -> 0%
where the time goes in v1:
time: 224 us; the launch traced here: 223 us
  blocking collectives  97.5 us (44%)
  waiting for transfers between devices  62.8 us (28%)
  matrix products  31.2 us (14%)
  local copies, waits for them, and re-layouts  15.9 us (7%)
  starting transfers between devices  8.24 us (4%)
  other arithmetic  7.31 us (3%)
    all_to_all x1, blocking collectives, shards(): lax.all_to_all(outbound, 'seq', split_axis=0, concat_axis=0, tiled=True)  51.7 us
    all_to_all x1, waiting for transfers between devices, shards(): lax.all_to_all(result.reshape(block_in.shape), 'seq', split_axis=0, conca...  49.1 us
    all_to_all x1, blocking collectives, shards(): got = lax.all_to_all(send, 'seq', split_axis=0, concat_axis=0, tiled=True)  45.8 us
    dot_general x1, matrix products, shards(): jnp.dot(hidden, expert_down[0], preferred_element_type=jnp.float32)  14.4 us
    all_to_all x1, waiting for transfers between devices, shards(): lax.all_to_all(mixed.reshape(devices, tokens, group_width), 'seq', split_...  13.7 us
    unnamed x23, local copies, waits for them, and re-layouts  9.77 us
    all_to_all x1, starting transfers between devices, shards(): lax.all_to_all(result.reshape(block_in.shape), 'seq', split_axis=0, conca...  4.68 us
  transfers between devices with their start and end apart: 2, of which 2 were waited for; matrix products, arithmetic and copies ran while one was open for 1% of the time, Pallas kernels for 0%

profile of v1, /device:TPU:0, one launch (start us, length us, event | category | flops | bytes accessed | tf_op | source)
XLA Modules:
  0.0 223.1 jit_solution(4223556259221613257)
XLA Ops:
  0.0 0.8 fusion.54
  0.8 0.7 fusion.53
  1.5 2.3 %copy.85 = bf16[128,4096]{0,1:T(8,128)(2,1)} copy(bf16[128,4096]{1,0:T(8,128)(2,1)} %param.13) | data formatting | bytes 2097152 | tf_op args[0]
  3.8 2.3 %copy.86 = bf16[128,4096]{0,1:T(8,128)(2,1)} copy(bf16[128,4096]{1,0:T(8,128)(2,1)} %param.14) | data formatting | bytes 2097152 | tf_op args[1]
  6.1 1.3 copy.87
  7.5 2.0 fusion.9
  9.5 4.0 %copy.94 = bf16[8,128,1664]{2,1,0:T(8,128)(2,1)} copy(bf16[8,128,1664]{1,2,0:T(8,128)(2,1)S(1)} %fusion.9) | data formatting | bytes 6815744 | tf_op jit(solution)/shard_map/concatenate | solution.py:63
  13.4 45.8 %all_to_all.20 = bf16[8,128,1664]{2,1,0:T(8,128)(2,1)S(1)} all-to-all(bf16[8,128,1664]{2,1,0:T(8,128)(2,1)} %copy.94), channel_id=1, replica_groups=mesh['seq'=8,'batch'=4] {'seq'}, dimensions={0} | all-to-all | bytes 6815744 | tf_op jit(solution)/shard_map/all_to_all | solution.py:72
  59.2 0.7 slice.82
  59.9 1.8 copy.100
  61.7 1.0 convert_element_type.86
  64.0 1.4 fusion.10
  65.4 2.4 %divide_convert_fusion = bf16[1024,512]{1,0:T(8,128)(2,1)} fusion(f32[1024]{0:T(1024)S(1)} %abs_maximum_fusion, bf16[1024,1664]{1,0:T(8,128)(2,1)S(1)} %bitcast.83, f32[1024,1024]{0,1:T(8,128)S(1)} %get-tuple-element.20, f32[1024]{0:T(1024)S(1)} %maximum_bitcast_fusion, f32[1024]{0:T(1024)S(1)} %bitcast_subtract_fusion.1), kind=kOutput, calls=%fused_computation.28 | convolution fusion | flops 1082130432 | bytes 6303744 | tf_op jit(solution)/shard_map/dot_general | solution.py:31
  67.8 3.6 %all-to-all-start.1 = ((bf16[8,128,512]{2,1,0:T(8,128)(2,1)}), bf16[8,128,512]{2,1,0:T(8,128)(2,1)S(1)}, u32[]{:S(2)}, u32[]{:S(2)}) async-start(bf16[8,128,512]{2,1,0:T(8,128)(2,1)} %bitcast.84), calls=%async_computation.1 | async-start | bytes 2097152 | tf_op jit(solution)/shard_map/all_to_all | solution.py:82
  73.0 13.7 %all-to-all-done.1 = bf16[8,128,512]{2,1,0:T(8,128)(2,1)S(1)} async-done(((bf16[8,128,512]{2,1,0:T(8,128)(2,1)}), bf16[8,128,512]{2,1,0:T(8,128)(2,1)S(1)}, u32[]{:S(2)}, u32[]{:S(2)}) %all-to-all-start.1) | async-done | bytes 1048608 | tf_op jit(solution)/shard_map/all_to_all | solution.py:82
  88.2 1.4 convolution_convert_fusion
  89.7 51.7 %all_to_all.21 = bf16[8,64,4096]{2,1,0:T(8,128)(2,1)S(1)} all-to-all(bf16[8,64,4096]{2,1,0:T(8,128)(2,1)S(1)} %bitcast.73), channel_id=1, replica_groups=mesh['seq'=8,'batch'=4] {'seq'}, dimensions={0} | all-to-all | bytes 8388608 | tf_op jit(solution)/shard_map/all_to_all | solution.py:109
  141.3 2.0 copy-done
  143.3 4.4 %fusion.4 = f32[512,704]{0,1:T(8,128)} fusion(bf16[512,4096]{1,0:T(8,128)(2,1)S(1)} %bitcast.79, bf16[1,4096,704]{1,2,0:T(8,128)(2,1)S(1)} %bitcast.89), kind=kOutput, calls=%fused_computation.7 | convolution fusion | flops 2952790016 | bytes 11403264 | tf_op jit(solution)/shard_map/dot_general | solution.py:111
  147.7 14.4 %convolution_convert_fusion.1 = bf16[512,4096]{1,0:T(8,128)(2,1)} fusion(bf16[1,704,4096]{2,1,0:T(8,128)(2,1)} %param.23, bf16[512,4096]{1,0:T(8,128)(2,1)} %bitcast.80, bf16[1,4096,704]{1,2,0:T(8,128)(2,1)} %param.22, f32[512,704]{0,1:T(8,128)} %fusion.4), kind=kOutput, calls=%fused_computation.3 | convolution fusion | flops 5909839872 | bytes 21364736 | tf_op jit(solution)/shard_map/dot_general | solution.py:114
  162.1 4.7 %all-to-all-start.3 = ((bf16[8,64,4096]{2,1,0:T(8,128)(2,1)}), bf16[8,64,4096]{2,1,0:T(8,128)(2,1)}, u32[]{:S(2)}, u32[]{:S(2)}) async-start(bf16[8,64,4096]{2,1,0:T(8,128)(2,1)} %bitcast.78), calls=%async_computation.3 | async-start | bytes 8388608 | tf_op jit(solution)/shard_map/all_to_all | solution.py:117
  166.8 49.1 %all-to-all-done.3 = bf16[8,64,4096]{2,1,0:T(8,128)(2,1)} async-done(((bf16[8,64,4096]{2,1,0:T(8,128)(2,1)}), bf16[8,64,4096]{2,1,0:T(8,128)(2,1)}, u32[]{:S(2)}, u32[]{:S(2)}) %all-to-all-start.3) | async-done | bytes 4194336 | tf_op jit(solution)/shard_map/all_to_all | solution.py:117
  215.9 2.9 %convolution_multiply_fusion.1 = f32[128,4096]{1,0:T(8,128)S(1)} fusion(bf16[512,4096]{1,0:T(8,128)(2,1)} %bitcast.31, f32[128]{0:T(128)S(1)} %get-tuple-element.16, s32[128]{0:T(128)S(1)} %get-tuple-element.17), kind=kOutput, calls=%fused_computation.12 | convolution fusion | flops 537460736 | bytes 6292480 | tf_op jit(solution)/shard_map/dot_general | solution.py:121
  218.8 4.3 %fusion.8 = bf16[128,4096]{1,0:T(8,128)(2,1)} fusion(f32[128,4096]{1,0:T(8,128)S(1)} %convolution_multiply_fusion.1, bf16[512,4096]{1,0:T(8,128)(2,1)} %bitcast.31, bf16[128,4096]{1,0:T(8,128)(2,1)S(1)} %get-tuple-element.6, f32[128]{0:T(128)S(1)} %get-tuple-element.15, s32[128]{0:T(128)S(1)} %get-tuple-element.18), kind=kOutput, calls=%fused_computation.13 | convolution fusion | flops 539557888 | bytes 8389632 | tf_op jit(solution)/shard_map/dot_general | solution.py:122
  (59 shorter events, 4.4 us)
Async XLA Ops:
  0.0 6.1 %copy-start.2 = (bf16[128,4096]{1,0:T(8,128)(2,1)S(1)}, bf16[128,4096]{1,0:T(8,128)(2,1)}, u32[]{:S(2)}) copy-start(bf16[128,4096]{1,0:T(8,128)(2,1)} %param.15) | copy-start | bytes 3145732
  65.4 6.0 %copy-start.5 = (s32[128,2]{0,1:T(2,128)S(1)}, s32[128,2]{0,1:T(2,128)}, u32[]{:S(2)}) copy-start(s32[128,2]{0,1:T(2,128)} %param.24) | copy-start | bytes 3076
  67.8 18.9 %all-to-all-start.1 = ((bf16[8,128,512]{2,1,0:T(8,128)(2,1)}), bf16[8,128,512]{2,1,0:T(8,128)(2,1)S(1)}, u32[]{:S(2)}, u32[]{:S(2)}) async-start(bf16[8,128,512]{2,1,0:T(8,128)(2,1)} %bitcast.84), calls=%async_computation.1 | async-start | bytes 2097152 | tf_op jit(solution)/shard_map/all_to_all | solution.py:82
  73.0 14.6 %copy-start.1 = (bf16[128,4096]{1,0:T(8,128)(2,1)S(1)}, bf16[128,4096]{1,0:T(8,128)(2,1)}, u32[]{:S(2)}) copy-start(bf16[128,4096]{1,0:T(8,128)(2,1)} %param.16) | copy-start | bytes 3145732
  73.0 14.6 %copy-start.3 = (f32[4096]{0:T(1024)S(1)}, f32[4096]{0:T(1024)}, u32[]{:S(2)}) copy-start(f32[4096]{0:T(1024)} %param.19) | copy-start | bytes 49156
  87.0 1.3 copy-start.4
  88.2 55.1 %slice-start = ((s8[5767168]{0:T(1024)(128)(4,1)}), s8[4194304]{0:T(1024)(128)(4,1)S(1)}, s32[]{:S(2)}) async-start(s8[5767168]{0:T(1024)(128)(4,1)} %bitcast.88), calls=%async_computation.4 | async-start | bytes 8388608
  89.6 53.6 %slice-start.1 = ((s8[5767168]{0:T(1024)(128)(4,1)}), s8[1572864]{0:T(1024)(128)(4,1)S(1)}, s32[]{:S(2)}) async-start(s8[5767168]{0:T(1024)(128)(4,1)} %bitcast.88), calls=%async_computation.5 | async-start | bytes 3145728
  141.3 2.0 copy-start
  162.1 4.7 %copy-start.6 = (f32[128,2]{0,1:T(2,128)S(1)}, f32[128,2]{0,1:T(2,128)}, u32[]{:S(2)}) copy-start(f32[128,2]{0,1:T(2,128)} %param.25) | copy-start | bytes 3076
  162.1 53.8 %all-to-all-start.3 = ((bf16[8,64,4096]{2,1,0:T(8,128)(2,1)}), bf16[8,64,4096]{2,1,0:T(8,128)(2,1)}, u32[]{:S(2)}, u32[]{:S(2)}) async-start(bf16[8,64,4096]{2,1,0:T(8,128)(2,1)} %bitcast.78), calls=%async_computation.3 | async-start | bytes 8388608 | tf_op jit(solution)/shard_map/all_to_all | solution.py:117

commit v2 on v1

--- a/solution.py
+++ b/solution.py
@@ -3,9 +3,12 @@
 import jax
 import jax.numpy as jnp
 from jax import lax
+from jax.experimental import pallas as pl
+from jax.experimental.pallas import tpu as pltpu
 from jax.sharding import PartitionSpec as P
 
 EPSILON = 1e-06
+PIECES = 4
 
 
 def three_parts(array):
@@ -30,6 +33,286 @@
     denom_sum = jnp.sum(coef, axis=1, keepdims=True)
     numer_sum = jnp.dot(coef.astype(jnp.bfloat16), value, preferred_element_type=jnp.float32)
     return numer_sum / jnp.maximum(jnp.abs(denom_sum), 1.0)
+
+
+def expert_kernel(
+    normed,
+    updated,
+    pick,
+    pick_back,
+    slot_weight,
+    gate_far,
+    up_far,
+    down_far,
+    out,
+    blocks,
+    gate,
+    up,
+    down,
+    rows,
+    gate_sum,
+    up_sum,
+    hidden,
+    core_out,
+    own,
+    core_in,
+    hop_out,
+    hop_in,
+    keep,
+    last_out,
+    last_in,
+    load_sem,
+    gather_send,
+    gather_recv,
+    core_send,
+    core_recv,
+    hop_send,
+    hop_recv,
+    last_send,
+    last_recv,
+):
+    me = lax.axis_index("seq")
+    width = rows.shape[1]
+    capacity = pick.shape[1]
+
+    def peer(flip):
+        total = 0
+        for bit in (1, 2, 4):
+            own_bit = lax.rem(lax.div(me, bit), 2)
+            total = total + bit * ((1 - own_bit) if flip & bit else own_bit)
+        return {"seq": total}
+
+    def remote(source, target, send_sem, recv_sem, flip):
+        return pltpu.make_async_remote_copy(
+            src_ref=source,
+            dst_ref=target,
+            send_sem=send_sem,
+            recv_sem=recv_sem,
+            device_id=peer(flip),
+            device_id_type=pl.DeviceIdType.MESH,
+        )
+
+    loads = [
+        pltpu.make_async_copy(far, near, load_sem.at[i])
+        for i, (far, near) in enumerate(((gate_far, gate), (up_far, up), (down_far, down)))
+    ]
+    for load in loads:
+        load.start()
+    barrier = pltpu.get_barrier_semaphore()
+    for flip in (1, 2, 4):
+        pl.semaphore_signal(
+            barrier, inc=1, device_id=peer(flip), device_id_type=pl.DeviceIdType.MESH
+        )
+    pl.semaphore_wait(barrier, 3)
+
+    def columns(piece):
+        return pl.ds(piece * width, width)
+
+    def block(slot, piece):
+        return normed.at[:, columns(piece)] if slot == 0 else blocks.at[slot - 1, piece]
+
+    gathers = {}
+    for piece in range(PIECES):
+        across = (4, 2) if piece % 2 == 0 else (2, 4)
+        for slot, source, flip in (
+            (1, 0, 1),
+            (2, 0, 2),
+            (4, 0, 4),
+            (6,) + across,
+            (3, 2, 1),
+            (5, 4, 1),
+            (7, 6, 1),
+        ):
+            gathers[slot, piece] = remote(
+                block(source, piece),
+                block(slot, piece),
+                gather_send.at[slot - 1, piece],
+                gather_recv.at[slot - 1, piece],
+                flip,
+            )
+
+    def send_own(piece):
+        for slot in (2, 4, 1):
+            gathers[slot, piece].start()
+
+    def first_products(piece):
+        for slot in (1, 3, 5, 7):
+            gathers[slot, piece].wait_recv()
+        if piece == 0:
+            loads[0].wait()
+            loads[1].wait()
+        for slot in range(8):
+            rows[slot * capacity : (slot + 1) * capacity, :] = jnp.dot(
+                pick[slot], block(slot, piece)[...], preferred_element_type=jnp.float32
+            ).astype(jnp.bfloat16)
+        for weight, total in ((gate, gate_sum), (up, up_sum)):
+            term = jnp.dot(
+                rows[...], weight[columns(piece), :], preferred_element_type=jnp.float32
+            )
+            total[...] = term if piece == 0 else total[...] + term
+
+    send_own(0)
+    send_own(1)
+    for piece in range(PIECES):
+        gathers[2, piece].wait_recv()
+        gathers[4, piece].wait_recv()
+        for slot in (6, 3, 5):
+            gathers[slot, piece].start()
+        if piece + 2 < PIECES:
+            send_own(piece + 2)
+        gathers[6, piece].wait_recv()
+        gathers[7, piece].start()
+        if piece > 0:
+            first_products(piece - 1)
+    first_products(PIECES - 1)
+    gate_val = gate_sum[...]
+    hidden[...] = (gate_val / (1.0 + jnp.exp(-gate_val)) * up_sum[...]).astype(jnp.bfloat16)
+    loads[2].wait()
+
+    core_copies, hop_copies, last_copies = {}, {}, {}
+
+    def second_product(piece):
+        rows[...] = (
+            jnp.dot(hidden[...], down[:, columns(piece)], preferred_element_type=jnp.float32)
+            * slot_weight[...]
+        ).astype(jnp.bfloat16)
+        for slot in (7, 5, 3, 1, 6, 4, 2, 0):
+            part = jnp.dot(
+                pick_back[slot],
+                rows[slot * capacity : (slot + 1) * capacity, :],
+                preferred_element_type=jnp.float32,
+            ).astype(jnp.bfloat16)
+            half = slot // 2
+            if slot % 2 == 0:
+                own[half, piece] = part
+                continue
+            core_out[half, piece] = part
+            core_copies[half, piece] = remote(
+                core_out.at[half, piece],
+                core_in.at[half, piece],
+                core_send.at[half, piece],
+                core_recv.at[half, piece],
+                1,
+            )
+            core_copies[half, piece].start()
+
+    def first_hop(piece):
+        first, second = (2, 4) if piece % 2 == 0 else (4, 2)
+        for slot in (6, first, second, 0):
+            half = slot // 2
+            core_copies[half, piece].wait_recv()
+            both = own[half, piece].astype(jnp.float32) + core_in[half, piece].astype(jnp.float32)
+            if slot in (0, second):
+                keep[0 if slot == 0 else 1, piece] = both
+                continue
+            place = 1 if slot == 6 else 0
+            hop_out[place, piece] = both.astype(jnp.bfloat16)
+            hop_copies[place, piece] = remote(
+                hop_out.at[place, piece],
+                hop_in.at[place, piece],
+                hop_send.at[place, piece],
+                hop_recv.at[place, piece],
+                first,
+            )
+            hop_copies[place, piece].start()
+
+    def second_hop(piece):
+        second = 4 if piece % 2 == 0 else 2
+        hop_copies[1, piece].wait_recv()
+        last_out[piece] = (keep[1, piece] + hop_in[1, piece].astype(jnp.float32)).astype(
+            jnp.bfloat16
+        )
+        last_copies[piece] = remote(
+            last_out.at[piece], last_in.at[piece], last_send.at[piece], last_recv.at[piece], second
+        )
+        last_copies[piece].start()
+
+    def finish(piece):
+        hop_copies[0, piece].wait_recv()
+        last_copies[piece].wait_recv()
+        out[:, columns(piece)] = (
+            updated[:, columns(piece)].astype(jnp.float32)
+            + (
+                keep[0, piece]
+                + hop_in[0, piece].astype(jnp.float32)
+                + last_in[piece].astype(jnp.float32)
+            )
+        ).astype(jnp.bfloat16)
+
+    for piece in range(PIECES):
+        second_product(piece)
+        if piece > 0:
+            first_hop(piece - 1)
+    first_hop(PIECES - 1)
+    for piece in range(PIECES):
+        second_hop(piece)
+        if piece > 0:
+            finish(piece - 1)
+    finish(PIECES - 1)
+    for copies in (gathers, core_copies, hop_copies, last_copies):
+        for copy in copies.values():
+            copy.wait_send()
+
+
+def cube_experts(normed, updated, pick, slot_weight, gate_weight, up_weight, down_weight):
+    tokens, model_width = normed.shape
+    hidden_width = gate_weight.shape[1]
+    slots = slot_weight.shape[0]
+    width = model_width // PIECES
+    near = pl.BlockSpec(memory_space=pltpu.VMEM)
+    far = pl.BlockSpec(memory_space=pl.ANY)
+
+    def pieces(*lead, kind=jnp.bfloat16):
+        return pltpu.VMEM(lead + (PIECES, tokens, width), kind)
+
+    def flags(*shape):
+        return pltpu.SemaphoreType.DMA(shape)
+
+    return pl.pallas_call(
+        expert_kernel,
+        out_shape=jax.ShapeDtypeStruct((tokens, model_width), jnp.bfloat16),
+        in_specs=[near] * 5 + [far] * 3,
+        out_specs=near,
+        scratch_shapes=[
+            pieces(7),
+            pltpu.VMEM(gate_weight.shape, jnp.bfloat16),
+            pltpu.VMEM(up_weight.shape, jnp.bfloat16),
+            pltpu.VMEM(down_weight.shape, jnp.bfloat16),
+            pltpu.VMEM((slots, width), jnp.bfloat16),
+            pltpu.VMEM((slots, hidden_width), jnp.float32),
+            pltpu.VMEM((slots, hidden_width), jnp.float32),
+            pltpu.VMEM((slots, hidden_width), jnp.bfloat16),
+            pieces(4),
+            pieces(4),
+            pieces(4),
+            pieces(2),
+            pieces(2),
+            pieces(2, kind=jnp.float32),
+            pieces(),
+            pieces(),
+            flags(3),
+            flags(7, PIECES),
+            flags(7, PIECES),
+            flags(4, PIECES),
+            flags(4, PIECES),
+            flags(2, PIECES),
+            flags(2, PIECES),
+            flags(PIECES),
+            flags(PIECES),
+        ],
+        compiler_params=pltpu.CompilerParams(
+            collective_id=1, has_side_effects=True, vmem_limit_bytes=67043328
+        ),
+    )(
+        normed,
+        updated,
+        pick,
+        jnp.transpose(pick, (0, 2, 1)),
+        slot_weight,
+        gate_weight,
+        up_weight,
+        down_weight,
+    )
 
 
 def shards(
@@ -58,8 +341,24 @@
         moved = jnp.transpose(array.reshape(tokens, head_count, head_dim), (1, 0, 2))
         return jnp.repeat(moved, group, axis=0)
 
+    capacity = 4 * tokens // devices
+    flat_routes = routes.reshape(-1)
+    matches = (flat_routes[:, None] == jnp.arange(devices, dtype=jnp.int32)[None, :]).astype(
+        jnp.int32
+    )
+    before = jnp.cumsum(matches, axis=0) - matches
+    position = jnp.sum(before * matches, axis=1)
+    position = position.reshape(tokens, 2)
+    slot_index = (flat_routes * capacity + position.reshape(-1)).reshape(tokens, 2)
     gates = jnp.stack(three_parts(input_logit) + three_parts(forget_logit), axis=2)
-    gates = jnp.pad(jnp.repeat(gates, group, axis=0), ((0, 0), (0, 0), (0, 122)))
+    gates = jnp.repeat(gates, group, axis=0)
+    notes = jnp.concatenate(
+        [routes.astype(jnp.bfloat16), position.astype(jnp.bfloat16)] + three_parts(route_weight),
+        axis=1,
+    )
+    notes = jnp.broadcast_to(notes[None], (devices,) + notes.shape)
+    gates = jnp.concatenate((gates, notes), axis=2)
+    gates = jnp.pad(gates, ((0, 0), (0, 0), (0, 128 - gates.shape[2])))
     send = jnp.concatenate(
         (
             by_head(queries),
@@ -91,14 +390,25 @@
     updated_float = updated.astype(jnp.float32)
     updated_square = jnp.mean(updated_float * updated_float, axis=1, keepdims=True)
     normed = (updated_float * lax.rsqrt(updated_square + EPSILON) * ffn_gain).astype(jnp.bfloat16)
-    capacity = 4 * tokens // devices
-    flat_routes = routes.reshape(-1)
-    matches = (flat_routes[:, None] == jnp.arange(devices, dtype=jnp.int32)[None, :]).astype(
-        jnp.int32
-    )
-    before = jnp.cumsum(matches, axis=0) - matches
-    position = jnp.sum(before * matches, axis=1)
-    slot_index = (flat_routes * capacity + position).reshape(tokens, 2)
+    if devices == 8:
+        me = lax.axis_index("seq")
+        told = gate_parts[:, 6:16].reshape(devices, tokens, 10)
+        told = told[jnp.bitwise_xor(me, jnp.arange(devices, dtype=jnp.int32))]
+        mine = me.astype(jnp.float32)
+        places = jnp.where(told[:, :, 0:2] == mine, told[:, :, 2:4], -1.0)
+        slots = jnp.arange(capacity, dtype=jnp.float32)[None, :, None]
+        pick_one = places[:, None, :, 0] == slots
+        pick_two = places[:, None, :, 1] == slots
+        weights = told[:, :, 4:6] + told[:, :, 6:8] + told[:, :, 8:10]
+        slot_weight = jnp.sum(
+            jnp.where(pick_one, weights[:, None, :, 0], 0.0)
+            + jnp.where(pick_two, weights[:, None, :, 1], 0.0),
+            axis=2,
+        ).reshape(devices * capacity, 1)
+        pick = jnp.logical_or(pick_one, pick_two).astype(jnp.bfloat16)
+        return cube_experts(
+            normed, updated, pick, slot_weight, expert_gate[0], expert_up[0], expert_down[0]
+        )
     columns = jnp.arange(devices * capacity, dtype=jnp.int32)
     pick_first = (slot_index[:, 0:1] == columns[None, :]).astype(jnp.bfloat16)
     pick_second = (slot_index[:, 1:2] == columns[None, :]).astype(jnp.bfloat16)

time: 224 us -> 193 us (0.86)
  blocking collectives: 97.5 us -> 0 us
  Pallas kernels: 0 us -> 94.6 us
  matrix products: 31.2 us -> 3.79 us
  waiting for transfers between devices: 62.8 us -> 35.4 us
  local copies, waits for them, and re-layouts: 15.9 us -> 37.4 us
  other arithmetic: 7.31 us -> 11.9 us
    all_to_all x2 -> x0, blocking collectives: 97.5 us -> none  [the longest x1 51.7 us: shards(): lax.all_to_all(outbound, 'seq', split_axis=0, concat_axis=0, tiled=True)]
    pallas_call x0 -> x1, Pallas kernels: none -> 94.6 us  [cube_experts(): pl.pallas_call(expert_kernel, out_shape=jax.ShapeDtypeStruct((tokens, mod...]
    dot_general x5 -> x0, matrix products: 27.4 us -> none  [the longest x1 14.4 us: shards(): jnp.dot(hidden, expert_down[0], preferred_element_type=jnp.float32)]
    all_to_all x1, waiting for transfers between devices: 49.1 us -> 23.7 us  [shards(): got = lax.all_to_all(send, 'seq', split_axis=0, concat_axis=0, tiled=True)]
    unnamed x23 -> x19, local copies, waits for them, and re-layouts: 9.77 us -> 28.7 us
    convert_element_type x0 -> x6, other arithmetic: none -> 4.5 us  [the longest x2 1.74 us: shards(): pick = jnp.logical_or(pick_one, pick_two).astype(jnp.bfloat16)]
  transfers between devices with their start and end apart: 2 -> 2, of which waited for: 2 -> 2; matrix products, arithmetic and copies ran while one was open for 1% -> 11% of each run, Pallas kernels for 0% -> 0%
where the time goes in v2:
time: 193 us; the launch traced here: 192 us
  Pallas kernels  94.6 us (49%)
  local copies, waits for them, and re-layouts  37.4 us (19%)
  waiting for transfers between devices  35.4 us (18%)
  other arithmetic  11.9 us (6%)
  starting transfers between devices  8.94 us (5%)
  matrix products  3.79 us (2%)
    pallas_call x1, Pallas kernels, cube_experts(): pl.pallas_call(expert_kernel, out_shape=jax.ShapeDtypeStruct((tokens, mod...  94.6 us
    unnamed x19, local copies, waits for them, and re-layouts  28.7 us
    all_to_all x1, waiting for transfers between devices, shards(): got = lax.all_to_all(send, 'seq', split_axis=0, concat_axis=0, tiled=True)  23.7 us
    all_to_all x1, waiting for transfers between devices, shards(): lax.all_to_all(mixed.reshape(devices, tokens, group_width), 'seq', split_...  11.7 us
    all_to_all x1, starting transfers between devices, shards(): got = lax.all_to_all(send, 'seq', split_axis=0, concat_axis=0, tiled=True)  5.2 us
    concatenate x1, local copies, waits for them, and re-layouts, shards(): jnp.concatenate((by_head(queries), by_head(key_vectors), jnp.transpose(va...  4.02 us
  transfers between devices with their start and end apart: 2, of which 2 were waited for; matrix products, arithmetic and copies ran while one was open for 11% of the time, Pallas kernels for 0%

profile of v2, /device:TPU:0, one launch (start us, length us, event | category | flops | bytes accessed | tf_op | source)
XLA Modules:
  0.0 192.3 jit_solution(13731053341727245734)
XLA Ops:
  0.0 0.8 convert_element_type.94
  0.8 0.8 copy.75
  5.2 2.3 %copy.72 = bf16[128,4096]{0,1:T(8,128)(2,1)} copy(bf16[128,4096]{1,0:T(8,128)(2,1)} %param.13) | data formatting | bytes 2097152 | tf_op args[0]
  7.5 2.3 %copy.73 = bf16[128,4096]{0,1:T(8,128)(2,1)} copy(bf16[128,4096]{1,0:T(8,128)(2,1)} %param.14) | data formatting | bytes 2097152 | tf_op args[1]
  9.8 1.3 copy.74
  11.3 2.0 %fusion.1 = bf16[8,128,1664]{1,2,0:T(8,128)(2,1)S(1)} fusion(bf16[8,128,16]{1,2,0:T(8,128)(2,1)S(1)} %concatenate.10, bf16[8,128,512]{1,2,0:T(8,128)(2,1)} %bitcast.63, bf16[8,128,512]{1,2,0:T(8,128)(2,1)} %bitcast.62, bf16[8,128,512]{1,2,0:T(8,128)(2,1)} %bitcast.61), kind=kLoop, calls=%fused_computation.5 | loop fusion | flops 17039360 | bytes 6586368 | tf_op jit(solution)/shard_map/concatenate | solution.py:362
  13.3 4.0 %copy.84 = bf16[8,128,1664]{2,1,0:T(8,128)(2,1)} copy(bf16[8,128,1664]{1,2,0:T(8,128)(2,1)S(1)} %fusion.1) | data formatting | bytes 6815744 | tf_op jit(solution)/shard_map/concatenate | solution.py:362
  17.4 5.2 %all-to-all-start = ((bf16[8,128,1664]{2,1,0:T(8,128)(2,1)}), bf16[8,128,1664]{2,1,0:T(8,128)(2,1)S(1)}, u32[]{:S(2)}, u32[]{:S(2)}) async-start(bf16[8,128,1664]{2,1,0:T(8,128)(2,1)} %copy.84), calls=%async_computation | async-start | bytes 6815744 | tf_op jit(solution)/shard_map/all_to_all | solution.py:371
  22.6 8.5 %copy.88 = bf16[1,4096,704]{2,1,0:T(8,128)(2,1)} copy(bf16[1,4096,704]{1,2,0:T(8,128)(2,1)} %param.21) | data formatting | bytes 11534336 | tf_op args[8]
  31.1 8.4 %copy.89 = bf16[1,4096,704]{2,1,0:T(8,128)(2,1)} copy(bf16[1,4096,704]{1,2,0:T(8,128)(2,1)} %param.22) | data formatting | bytes 11534336 | tf_op args[9]
  39.5 23.7 %all-to-all-done = bf16[8,128,1664]{2,1,0:T(8,128)(2,1)S(1)} async-done(((bf16[8,128,1664]{2,1,0:T(8,128)(2,1)}), bf16[8,128,1664]{2,1,0:T(8,128)(2,1)S(1)}, u32[]{:S(2)}, u32[]{:S(2)}) %all-to-all-start) | async-done | bytes 3407904 | tf_op jit(solution)/shard_map/all_to_all | solution.py:371
  63.9 1.8 copy.91
  65.7 0.8 slice.121
  66.5 1.0 convert_element_type.102
  68.9 1.4 fusion.2
  70.2 2.4 %divide_convert_fusion = bf16[1024,512]{1,0:T(8,128)(2,1)} fusion(f32[1024]{0:T(1024)S(1)} %abs_maximum_fusion, bf16[1024,1664]{1,0:T(8,128)(2,1)S(1)} %bitcast.66, f32[1024,1024]{0,1:T(8,128)S(1)} %get-tuple-element.25, f32[1024]{0:T(1024)S(1)} %maximum_bitcast_fusion, f32[1024]{0:T(1024)S(1)} %bitcast_subtract_fusion.1), kind=kOutput, calls=%fused_computation.17 | convolution fusion | flops 1082130432 | bytes 6303744 | tf_op jit(solution)/shard_map/dot_general | solution.py:34
  72.7 3.7 %all-to-all-start.1 = ((bf16[8,128,512]{2,1,0:T(8,128)(2,1)}), bf16[8,128,512]{2,1,0:T(8,128)(2,1)S(1)}, u32[]{:S(2)}, u32[]{:S(2)}) async-start(bf16[8,128,512]{2,1,0:T(8,128)(2,1)} %bitcast.67), calls=%async_computation.1 | async-start | bytes 2097152 | tf_op jit(solution)/shard_map/all_to_all | solution.py:381
  77.2 0.9 reshape.179.slot_weight
  78.8 1.0 fusion.19.pick_back
  79.9 11.7 %all-to-all-done.1 = bf16[8,128,512]{2,1,0:T(8,128)(2,1)S(1)} async-done(((bf16[8,128,512]{2,1,0:T(8,128)(2,1)}), bf16[8,128,512]{2,1,0:T(8,128)(2,1)S(1)}, u32[]{:S(2)}, u32[]{:S(2)}) %all-to-all-start.1) | async-done | bytes 1048608 | tf_op jit(solution)/shard_map/all_to_all | solution.py:381
  93.1 1.0 copy-done
  94.1 1.3 fusion.6.normed
  95.4 94.6 %shard_map.127 = bf16[128,4096]{1,0:T(8,128)(2,1)} custom-call(bf16[128,4096]{1,0:T(8,128)(2,1)} %fusion.6.normed, bf16[128,4096]{1,0:T(8,128)(2,1)} %copy-done, bf16[8,64,128]{2,1,0:T(8,128)(2,1)} %fusion.21.pick, bf16[8,128,64]{2,1,0:T(8,128)(2,1)} %fusion.19.pick_back, f32[512,1]{1,0:T(8,128)} %reshape.179.slot_weight, bf16[4096,704]{1,0:T(8,128)(2,1)} %bitcast.57, ...), custom_call_target="tpu_custom_call" | custom-call | tf_op jit(solution)/shard_map/pallas_call | solution.py:271
  190.0 2.3 %copy.95 = bf16[128,4096]{1,0:T(8,128)(2,1)} copy(bf16[128,4096]{1,0:T(8,128)(2,1)} %shard_map.127) | data formatting | bytes 2097152
  (63 shorter events, 8.8 us)
Async XLA Ops:
  0.0 9.8 %copy-start.2 = (bf16[128,4096]{1,0:T(8,128)(2,1)S(1)}, bf16[128,4096]{1,0:T(8,128)(2,1)}, u32[]{:S(2)}) copy-start(bf16[128,4096]{1,0:T(8,128)(2,1)} %param.15) | copy-start | bytes 3145732
  17.4 45.9 %all-to-all-start = ((bf16[8,128,1664]{2,1,0:T(8,128)(2,1)}), bf16[8,128,1664]{2,1,0:T(8,128)(2,1)S(1)}, u32[]{:S(2)}, u32[]{:S(2)}) async-start(bf16[8,128,1664]{2,1,0:T(8,128)(2,1)} %copy.84), calls=%async_computation | async-start | bytes 6815744 | tf_op jit(solution)/shard_map/all_to_all | solution.py:371
  72.7 18.9 %all-to-all-start.1 = ((bf16[8,128,512]{2,1,0:T(8,128)(2,1)}), bf16[8,128,512]{2,1,0:T(8,128)(2,1)S(1)}, u32[]{:S(2)}, u32[]{:S(2)}) async-start(bf16[8,128,512]{2,1,0:T(8,128)(2,1)} %bitcast.67), calls=%async_computation.1 | async-start | bytes 2097152 | tf_op jit(solution)/shard_map/all_to_all | solution.py:381
  79.8 12.5 %copy-start.1 = (bf16[128,4096]{1,0:T(8,128)(2,1)S(1)}, bf16[128,4096]{1,0:T(8,128)(2,1)}, u32[]{:S(2)}) copy-start(bf16[128,4096]{1,0:T(8,128)(2,1)} %param.16) | copy-start | bytes 3145732
  79.8 12.5 %copy-start.3 = (f32[4096]{0:T(1024)S(1)}, f32[4096]{0:T(1024)}, u32[]{:S(2)}) copy-start(f32[4096]{0:T(1024)} %param.19) | copy-start | bytes 49156
  92.1 2.0 %copy-start.4 = (f32[4096]{0:T(1024)S(1)}, f32[4096]{0:T(1024)}, u32[]{:S(2)}) copy-start(f32[4096]{0:T(1024)} %param.20) | copy-start | bytes 49156
  93.1 1.1 copy-start

commit v3 on v2

--- a/solution.py
+++ b/solution.py
@@ -1,3 +1,4 @@
+import functools
 import math
 
 import jax
@@ -11,12 +12,56 @@
 PIECES = 4
 
 
-def three_parts(array):
-    high = lax.reduce_precision(array, 8, 7)
-    rest = array - high
-    middle = lax.reduce_precision(rest, 8, 7)
-    low = rest - middle
-    return [part.astype(jnp.bfloat16) for part in (high, middle, low)]
+def exchange_kernel(moves, devices, *refs):
+    count = len(moves)
+    sources, targets = refs[:count], refs[count : 2 * count]
+    send_sem, recv_sem, local_sem = refs[2 * count :]
+    me = lax.axis_index("seq")
+    others = [lax.rem(me + step, devices) for step in range(1, devices)]
+    barrier = pltpu.get_barrier_semaphore()
+    for other in others:
+        pl.semaphore_signal(
+            barrier, inc=1, device_id={"seq": other}, device_id_type=pl.DeviceIdType.MESH
+        )
+    pl.semaphore_wait(barrier, devices - 1)
+    copies = []
+    for i, (take, put) in enumerate(moves):
+        for step, other in enumerate(others):
+            copies.append(
+                pltpu.make_async_remote_copy(
+                    src_ref=take(sources[i], other),
+                    dst_ref=put(targets[i], me),
+                    send_sem=send_sem.at[i, step],
+                    recv_sem=recv_sem.at[i, step],
+                    device_id={"seq": other},
+                    device_id_type=pl.DeviceIdType.MESH,
+                )
+            )
+            copies[-1].start()
+    for i, (take, put) in enumerate(moves):
+        copies.append(
+            pltpu.make_async_copy(take(sources[i], me), put(targets[i], me), local_sem.at[i])
+        )
+        copies[-1].start()
+    for copy in copies:
+        copy.wait()
+
+
+def exchange(moves, devices, number, sources, shapes):
+    far = pl.BlockSpec(memory_space=pl.ANY)
+    count = len(moves)
+    return pl.pallas_call(
+        functools.partial(exchange_kernel, moves, devices),
+        out_shape=shapes,
+        in_specs=[far] * count,
+        out_specs=[far] * count,
+        scratch_shapes=[
+            pltpu.SemaphoreType.DMA((count, devices - 1)),
+            pltpu.SemaphoreType.DMA((count, devices - 1)),
+            pltpu.SemaphoreType.DMA((count,)),
+        ],
+        compiler_params=pltpu.CompilerParams(collective_id=number, has_side_effects=True),
+    )(*sources)
 
 
 def head_mix(query, key, value, input_gate, forget_gate):
@@ -146,8 +191,11 @@
                 pick[slot], block(slot, piece)[...], preferred_element_type=jnp.float32
             ).astype(jnp.bfloat16)
         for weight, total in ((gate, gate_sum), (up, up_sum)):
-            term = jnp.dot(
-                rows[...], weight[columns(piece), :], preferred_element_type=jnp.float32
+            term = lax.dot_general(
+                rows[...],
+                weight[:, columns(piece)],
+                (((1,), (1,)), ((), ())),
+                preferred_element_type=jnp.float32,
             )
             total[...] = term if piece == 0 else total[...] + term
 
@@ -256,7 +304,7 @@
 
 def cube_experts(normed, updated, pick, slot_weight, gate_weight, up_weight, down_weight):
     tokens, model_width = normed.shape
-    hidden_width = gate_weight.shape[1]
+    hidden_width = gate_weight.shape[0]
     slots = slot_weight.shape[0]
     width = model_width // PIECES
     near = pl.BlockSpec(memory_space=pltpu.VMEM)
@@ -337,10 +385,6 @@
     group = devices // head_count
     group_width = model_width // devices
 
-    def by_head(array):
-        moved = jnp.transpose(array.reshape(tokens, head_count, head_dim), (1, 0, 2))
-        return jnp.repeat(moved, group, axis=0)
-
     capacity = 4 * tokens // devices
     flat_routes = routes.reshape(-1)
     matches = (flat_routes[:, None] == jnp.arange(devices, dtype=jnp.int32)[None, :]).astype(
@@ -350,38 +394,56 @@
     position = jnp.sum(before * matches, axis=1)
     position = position.reshape(tokens, 2)
     slot_index = (flat_routes * capacity + position.reshape(-1)).reshape(tokens, 2)
-    gates = jnp.stack(three_parts(input_logit) + three_parts(forget_logit), axis=2)
-    gates = jnp.repeat(gates, group, axis=0)
-    notes = jnp.concatenate(
-        [routes.astype(jnp.bfloat16), position.astype(jnp.bfloat16)] + three_parts(route_weight),
-        axis=1,
-    )
-    notes = jnp.broadcast_to(notes[None], (devices,) + notes.shape)
-    gates = jnp.concatenate((gates, notes), axis=2)
-    gates = jnp.pad(gates, ((0, 0), (0, 0), (0, 128 - gates.shape[2])))
-    send = jnp.concatenate(
+    notes = jnp.stack(
+        (jnp.repeat(input_logit, group, axis=0), jnp.repeat(forget_logit, group, axis=0)), axis=1
+    )
+    routing = jnp.concatenate(
+        (routes.astype(jnp.float32), position.astype(jnp.float32), route_weight), axis=1
+    )
+    routing = jnp.broadcast_to(jnp.transpose(routing)[None], (devices, 6, tokens))
+    notes = jnp.concatenate((notes, routing), axis=1)
+
+    def columns_of(width, share):
+        return lambda ref, other: ref.at[
+            :, pl.ds(pl.multiple_of((other // share) * width, width), width)
+        ]
+
+    def rows_from(ref, origin):
+        return ref.at[pl.ds(pl.multiple_of(origin * tokens, tokens), tokens), :]
+
+    def entry(ref, other):
+        return ref.at[other]
+
+    head_columns = columns_of(head_dim, group)
+    own_columns = columns_of(group_width, 1)
+    tall = devices * tokens
+    told, key_all, query_all, value_all = exchange(
         (
-            by_head(queries),
-            by_head(key_vectors),
-            jnp.transpose(value_vectors.reshape(tokens, devices, group_width), (1, 0, 2)),
-            gates,
+            (entry, entry),
+            (head_columns, rows_from),
+            (head_columns, rows_from),
+            (own_columns, rows_from),
         ),
-        axis=2,
-    )
-    got = lax.all_to_all(send, "seq", split_axis=0, concat_axis=0, tiled=True)
-    got = got.reshape(devices * tokens, -1)
-    gate_parts = got[:, 2 * head_dim + group_width :].astype(jnp.float32)
+        devices,
+        2,
+        (notes, key_vectors, queries, value_vectors),
+        (
+            jax.ShapeDtypeStruct(notes.shape, jnp.float32),
+            jax.ShapeDtypeStruct((tall, head_dim), jnp.bfloat16),
+            jax.ShapeDtypeStruct((tall, head_dim), jnp.bfloat16),
+            jax.ShapeDtypeStruct((tall, group_width), jnp.bfloat16),
+        ),
+    )
     mixed = head_mix(
-        got[:, :head_dim],
-        got[:, head_dim : 2 * head_dim],
-        got[:, 2 * head_dim : 2 * head_dim + group_width],
-        gate_parts[:, 0] + gate_parts[:, 1] + gate_parts[:, 2],
-        gate_parts[:, 3] + gate_parts[:, 4] + gate_parts[:, 5],
+        query_all, key_all, value_all, told[:, 0].reshape(-1), told[:, 1].reshape(-1)
     ).astype(jnp.bfloat16)
-    mixer_out = lax.all_to_all(
-        mixed.reshape(devices, tokens, group_width), "seq", split_axis=0, concat_axis=0, tiled=True
-    )
-    mixer_out = jnp.transpose(mixer_out, (1, 0, 2)).reshape(tokens, model_width)
+    (mixer_out,) = exchange(
+        ((rows_from, own_columns),),
+        devices,
+        3,
+        (mixed,),
+        (jax.ShapeDtypeStruct((tokens, model_width), jnp.bfloat16),),
+    )
     mixer_out = mixer_out.astype(jnp.float32)
     mixer_square = jnp.mean(mixer_out * mixer_out, axis=1, keepdims=True)
     updated = (
@@ -392,22 +454,25 @@
     normed = (updated_float * lax.rsqrt(updated_square + EPSILON) * ffn_gain).astype(jnp.bfloat16)
     if devices == 8:
         me = lax.axis_index("seq")
-        told = gate_parts[:, 6:16].reshape(devices, tokens, 10)
         told = told[jnp.bitwise_xor(me, jnp.arange(devices, dtype=jnp.int32))]
         mine = me.astype(jnp.float32)
-        places = jnp.where(told[:, :, 0:2] == mine, told[:, :, 2:4], -1.0)
+        places = jnp.where(told[:, 2:4] == mine, told[:, 4:6], -1.0)
         slots = jnp.arange(capacity, dtype=jnp.float32)[None, :, None]
-        pick_one = places[:, None, :, 0] == slots
-        pick_two = places[:, None, :, 1] == slots
-        weights = told[:, :, 4:6] + told[:, :, 6:8] + told[:, :, 8:10]
+        pick_one = places[:, 0:1] == slots
+        pick_two = places[:, 1:2] == slots
         slot_weight = jnp.sum(
-            jnp.where(pick_one, weights[:, None, :, 0], 0.0)
-            + jnp.where(pick_two, weights[:, None, :, 1], 0.0),
+            jnp.where(pick_one, told[:, 6:7], 0.0) + jnp.where(pick_two, told[:, 7:8], 0.0),
             axis=2,
         ).reshape(devices * capacity, 1)
         pick = jnp.logical_or(pick_one, pick_two).astype(jnp.bfloat16)
         return cube_experts(
-            normed, updated, pick, slot_weight, expert_gate[0], expert_up[0], expert_down[0]
+            normed,
+            updated,
+            pick,
+            slot_weight,
+            jnp.transpose(expert_gate[0]),
+            jnp.transpose(expert_up[0]),
+            expert_down[0],
         )
     columns = jnp.arange(devices * capacity, dtype=jnp.int32)
     pick_first = (slot_index[:, 0:1] == columns[None, :]).astype(jnp.bfloat16)

time: 193 us -> 178 us (0.922)
  Pallas kernels: 94.6 us -> 153 us
  waiting for transfers between devices: 35.4 us -> 0 us
  local copies, waits for them, and re-layouts: 37.4 us -> 6.64 us
  starting transfers between devices: 8.94 us -> 0 us
    pallas_call x0 -> x2, Pallas kernels: none -> 54.4 us  [exchange(): pl.pallas_call(functools.partial(exchange_kernel, moves, devices), out_sh...]
    all_to_all x2 -> x0, waiting for transfers between devices: 35.4 us -> none  [the longest x1 23.7 us: shards(): got = lax.all_to_all(send, 'seq', split_axis=0, concat_axis=0, tiled=True)]
    unnamed x19 -> x14, local copies, waits for them, and re-layouts: 28.7 us -> 4.07 us
    all_to_all x2 -> x0, starting transfers between devices: 8.94 us -> none  [the longest x1 5.2 us: shards(): got = lax.all_to_all(send, 'seq', split_axis=0, concat_axis=0, tiled=True)]
    concatenate x3 -> x0, local copies, waits for them, and re-layouts: 4.28 us -> none  [the longest x1 4.02 us: shards(): jnp.concatenate((by_head(queries), by_head(key_vectors), jnp.transpose(va...]
    pallas_call x1, Pallas kernels: 94.6 us -> 98.9 us  [cube_experts(): pl.pallas_call(expert_kernel, out_shape=jax.ShapeDtypeStruct((tokens, mod...]
  transfers between devices with their start and end apart: 2 -> 0, of which waited for: 2 -> 0; matrix products, arithmetic and copies ran while one was open for 11% -> 0% of each run, Pallas kernels for 0% -> 0%
where the time goes in v3:
time: 178 us; the launch traced here: 177 us
  Pallas kernels  153 us (86%)
  other arithmetic  11.9 us (7%)
  local copies, waits for them, and re-layouts  6.64 us (4%)
  matrix products  5.41 us (3%)
    pallas_call x1, Pallas kernels, cube_experts(): pl.pallas_call(expert_kernel, out_shape=jax.ShapeDtypeStruct((tokens, mod...  98.9 us
    pallas_call x2, Pallas kernels, exchange(): pl.pallas_call(functools.partial(exchange_kernel, moves, devices), out_sh...  54.4 us
    unnamed x14, local copies, waits for them, and re-layouts  4.07 us

profile of v3, /device:TPU:0, one launch (start us, length us, event | category | flops | bytes accessed | tf_op | source)
XLA Modules:
  0.0 177.4 jit_solution(14110054549959572356)
XLA Ops:
  0.0 0.8 copy.20
  0.9 0.6 reduce-window.24
  1.5 0.2 slice_reduce_fusion
  2.2 0.7 convert_element_type.46
  2.9 0.7 maximum_bitcast_fusion
  3.6 1.3 pad_maximum_fusion.refs_0_
  5.0 39.4 %shard_map.127 = (f32[8,8,128]{2,1,0:T(8,128)}, bf16[1024,512]{1,0:T(8,128)(2,1)}, bf16[1024,512]{1,0:T(8,128)(2,1)}, bf16[1024,512]{1,0:T(8,128)(2,1)}) custom-call(f32[8,8,128]{2,1,0:T(8,128)} %pad_maximum_fusion.refs_0_, bf16[128,4096]{1,0:T(8,128)(2,1)} %refs_1_.1, bf16[128,4096]{1,0:T(8,128)(2,1)} %refs_2_.1, bf16[128,4096]{1,0:T(8,128)(2,1)} %refs_3_.1), custom_call_target="tpu_custom_call" | custom-call | tf_op jit(solution)/shard_map/pallas_call | solution.py:53
  44.4 0.8 slice_negate_fusion
  45.3 0.3 reduce-window.26
  45.9 0.3 reduce-window.36
  46.5 3.0 %fusion = (f32[1024]{0:T(1024)S(1)}, f32[1024,1024]{0,1:T(8,128)S(1)}) fusion(f32[1024]{0:T(1024)S(1)} %maximum_bitcast_fusion.1, f32[1024]{0:T(1024)S(1)} %bitcast_subtract_fusion.1, bf16[1024,512]{1,0:T(8,128)(2,1)} %get-tuple-element.10, bf16[1024,512]{1,0:T(8,128)(2,1)} %get-tuple-element.11), kind=kOutput, calls=%fused_computation.7 | convolution fusion | flops 1081080832 | bytes 6303744 | tf_op jit(solution)/shard_map/dot_general | solution.py:72
  49.6 2.4 %divide_convert_fusion.refs_0_ = bf16[1024,512]{1,0:T(8,128)(2,1)} fusion(f32[1024]{0:T(1024)S(1)} %abs_maximum_fusion, bf16[1024,512]{1,0:T(8,128)(2,1)S(1)} %copy-done.5, f32[1024,1024]{0,1:T(8,128)S(1)} %get-tuple-element.22, f32[1024]{0:T(1024)S(1)} %maximum_bitcast_fusion.1, f32[1024]{0:T(1024)S(1)} %bitcast_subtract_fusion.1), kind=kOutput, calls=%fused_computation.16 | convolution fusion | flops 1082130432 | bytes 6303744 | tf_op jit(solution)/shard_map/dot_general | solution.py:79
  52.0 15.0 %shard_map.128 = bf16[128,4096]{1,0:T(8,128)(2,1)} custom-call(bf16[1024,512]{1,0:T(8,128)(2,1)} %divide_convert_fusion.refs_0_), custom_call_target="tpu_custom_call" | custom-call | tf_op jit(solution)/shard_map/pallas_call | solution.py:53
  67.0 1.5 fusion.2
  68.5 2.0 %fusion.6 = (f32[128]{0:T(128)S(1)}, bf16[128,4096]{1,0:T(8,128)(2,1)S(1)}) fusion(f32[4096]{0:T(1024)S(1)} %copy-done.3, f32[128]{0:T(128)S(1)} %add_rsqrt_fusion.1, bf16[128,4096]{1,0:T(8,128)(2,1)} %shard_map.128, bf16[128,4096]{1,0:T(8,128)(2,1)S(1)} %copy-done.1), kind=kLoop, calls=%fused_computation.13 | loop fusion | flops 4718464 | bytes 3163136 | tf_op jit(solution)/shard_map/reduce_sum | solution.py:453
  70.5 1.0 copy-done
  71.5 1.3 fusion.8.normed
  72.8 0.6 gather_fusion
  73.4 0.1 add_reduce_fusion
  73.6 0.9 reshape.127.slot_weight
  74.5 1.1 fusion.14.pick_back
  75.6 0.7 fusion.16.pick
  76.2 98.9 %shard_map.129 = bf16[128,4096]{1,0:T(8,128)(2,1)} custom-call(bf16[128,4096]{1,0:T(8,128)(2,1)} %fusion.8.normed, bf16[128,4096]{1,0:T(8,128)(2,1)} %copy-done, bf16[8,64,128]{2,1,0:T(8,128)(2,1)} %fusion.16.pick, bf16[8,128,64]{2,1,0:T(8,128)(2,1)} %fusion.14.pick_back, f32[512,1]{1,0:T(8,128)} %reshape.127.slot_weight, bf16[704,4096]{1,0:T(8,128)(2,1)} %bitcast.35, ...), custom_call_target="tpu_custom_call" | custom-call | tf_op jit(solution)/shard_map/pallas_call | solution.py:319
  175.1 2.3 %copy.25 = bf16[128,4096]{1,0:T(8,128)(2,1)} copy(bf16[128,4096]{1,0:T(8,128)(2,1)} %shard_map.129) | data formatting | bytes 2097152
  (39 shorter events, 1.4 us)
Async XLA Ops:
  46.5 3.0 %copy-start.5 = (bf16[1024,512]{1,0:T(8,128)(2,1)S(1)}, bf16[1024,512]{1,0:T(8,128)(2,1)}, u32[]{:S(2)}) copy-start(bf16[1024,512]{1,0:T(8,128)(2,1)} %get-tuple-element.12) | copy-start | bytes 3145732
  49.5 19.0 %copy-start.1 = (bf16[128,4096]{1,0:T(8,128)(2,1)S(1)}, bf16[128,4096]{1,0:T(8,128)(2,1)}, u32[]{:S(2)}) copy-start(bf16[128,4096]{1,0:T(8,128)(2,1)} %param.16) | copy-start | bytes 3145732
  49.5 19.0 %copy-start.3 = (f32[4096]{0:T(1024)S(1)}, f32[4096]{0:T(1024)}, u32[]{:S(2)}) copy-start(f32[4096]{0:T(1024)} %param.19) | copy-start | bytes 49156
  52.0 19.5 %copy-start.4 = (f32[4096]{0:T(1024)S(1)}, f32[4096]{0:T(1024)}, u32[]{:S(2)}) copy-start(f32[4096]{0:T(1024)} %param.20) | copy-start | bytes 49156
  52.0 20.8 %copy-start.2 = (f32[8,8,128]{2,1,0:T(8,128)S(1)}, f32[8,8,128]{2,1,0:T(8,128)}, u32[]{:S(2)}) copy-start(f32[8,8,128]{2,1,0:T(8,128)} %get-tuple-element.9) | copy-start | bytes 98308
  70.5 1.0 copy-start
